TPU v7x, 32 devices: a whole 2x2x4 slice. The times are simulated.
32 devices in a mesh: fsdp: 2 (over x), context: 4 (over z), tensor: 4 (over y, core).
Axes of the slice: x: 2, y: 2, z: 4, core: 2. Of those that a mesh axis runs over, the one named last changes fastest.
Arguments:
- activations: bfloat16 [2, 2048, 1152], P('fsdp', 'context'), may hold values from -6 to 6
- positions: int32 [2, 2048], P('fsdp', 'context'), may hold values from 0 to 2047, as said below
- seg_ids: int32 [2, 2048], P('fsdp', 'context'), may hold values from 0 to 3, as said below
- norm_gains: bfloat16 [4, 1152], P(None, ('fsdp', 'context')), may hold values from 0.5 to 1.5
- head_gains: bfloat16 [2, 256], P(None, ('fsdp', 'context')), may hold values from 0.25 to 1.75
- w_query: bfloat16 [1152, 1024], P(('fsdp', 'context'), 'tensor'), may hold values from -0.1875 to 0.1875
- w_keyval: bfloat16 [1152, 512], P(('fsdp', 'context')), may hold values from -0.1875 to 0.1875
- w_out: bfloat16 [1152, 1024], P(('fsdp', 'context'), 'tensor'), may hold values from -0.1875 to 0.1875
- w_gateup: bfloat16 [1152, 2, 6912], P(('fsdp', 'context'), None, 'tensor'), may hold values from -0.1875 to 0.1875
- w_down: bfloat16 [1152, 6912], P(('fsdp', 'context'), 'tensor'), may hold values from -0.078125 to 0.078125
- cotangent: bfloat16 [2, 2048, 1152], P('fsdp', 'context'), may hold values from -6 to 6
Outputs:
- block_output: bfloat16 [2, 2048, 1152], P('fsdp', 'context')
- input_grad: bfloat16 [2, 2048, 1152], P('fsdp', 'context')
- norm_gains_grad: float32 [4, 1152], P(None, ('fsdp', 'context'))
- head_gains_grad: float32 [2, 256], P(None, ('fsdp', 'context'))
- w_query_grad: float32 [1152, 1024], P(('fsdp', 'context'), 'tensor')
- w_keyval_grad: float32 [1152, 512], P(('fsdp', 'context'))
- w_out_grad: float32 [1152, 1024], P(('fsdp', 'context'), 'tensor')
- w_gateup_grad: float32 [1152, 2, 6912], P(('fsdp', 'context'), None, 'tensor')
- w_down_grad: float32 [1152, 6912], P(('fsdp', 'context'), 'tensor')
Inputs may be any that keep to these rules, and one draw needn't show every extreme that they name: `positions`: within a sequence, a document is a run of consecutive tokens with one document number; numbers never fall along a sequence. Positions are 0 at a document's first token and rise by one from token to token inside it. The first sequence is one document. `seg_ids`: document numbers of a sequence start at 0 and never fall along it.
All inputs are finite; a program needn't handle non-finite values.
Results may differ from a plain program's by a relative error of at most 0.024.
Values may be sent and summed in bfloat16 or wider, within the bound.
A program may use at most 192 MiB of HBM per device.

v0:
```python
import jax
import jax.numpy as jnp
from jax import lax
from jax.sharding import PartitionSpec as P

HD = 256
WINDOW = 512
EPSILON = 1e-06


def from_behind(block, axis, distance):
    devices = range(lax.axis_size(axis))
    route = [(i - distance, i) for i in devices if i - distance in devices]
    return lax.ppermute(block, axis, route)


def rms_norm(values, gain):
    factor = lax.rsqrt(jnp.mean(values * values, axis=-1, keepdims=True) + EPSILON)
    return values * factor * gain


def rotate(tensor, places):
    width_all = tensor.shape[-1]
    half_width = width_all // 2
    freqs = jnp.power(10000.0, -jnp.arange(half_width, dtype=jnp.float32) * 2.0 / width_all)
    angles = places.astype(jnp.float32)[:, None] * freqs[None, :]
    cosine = jnp.cos(angles)[:, None, :]
    sine = jnp.sin(angles)[:, None, :]
    first_half = tensor[..., :half_width]
    second_half = tensor[..., half_width:]
    return jnp.concatenate(
        [first_half * cosine - second_half * sine, second_half * cosine + first_half * sine],
        axis=-1,
    )


def glu(gate_up):
    return jax.nn.gelu(gate_up[:, 0], approximate=True) * gate_up[:, 1]


def contract_last(left_side, right_side):
    return lax.dot_general(
        left_side, right_side, (((1,), (1,)), ((), ())), preferred_element_type=jnp.float32
    )


def contract_first(left_side, right_side):
    return lax.dot_general(
        left_side, right_side, (((0,), (0,)), ((), ())), preferred_element_type=jnp.float32
    )


def shards(
    activations,
    positions,
    seg_ids,
    norm_gains,
    head_gains,
    w_query,
    w_keyval,
    w_out,
    w_gateup,
    w_down,
    cotangent,
):
    tokens = activations.shape[1]
    local_heads = w_query.shape[1] // HD
    inputs = activations[0].astype(jnp.float32)
    places = positions[0]
    documents = seg_ids[0]
    gains_all, heads_all, query_all, keyval_all, out_all = (
        lax.all_gather(norm_gains, ("fsdp", "context"), axis=1, tiled=True),
        lax.all_gather(head_gains, ("fsdp", "context"), axis=1, tiled=True),
        lax.all_gather(w_query, ("fsdp", "context"), axis=0, tiled=True),
        lax.all_gather(w_keyval, ("fsdp", "context"), axis=0, tiled=True),
        lax.all_gather(w_out, ("fsdp", "context"), axis=0, tiled=True),
    )
    gains_f = gains_all.astype(jnp.float32)
    heads_f = heads_all.astype(jnp.float32)
    normed_f, input_back = jax.vjp(rms_norm, inputs, gains_f[0])
    normed = normed_f.astype(jnp.bfloat16)
    query_raw = jnp.dot(normed, query_all, preferred_element_type=jnp.float32).reshape(
        tokens, local_heads, HD
    )
    keyval_raw = jnp.dot(normed, keyval_all, preferred_element_type=jnp.float32)

    def prepare(raw_heads, head_gain):
        return rotate(rms_norm(raw_heads, head_gain), places)

    query_rot, query_back = jax.vjp(prepare, query_raw, heads_f[0])
    key_rot, key_back = jax.vjp(prepare, keyval_raw[:, None, :HD], heads_f[1])
    queries = query_rot.astype(jnp.bfloat16)
    own_keyval = jnp.concatenate([key_rot[:, 0], keyval_raw[:, HD:]], axis=1).astype(jnp.bfloat16)
    labels = jnp.stack([places, documents])
    keep_from = tokens - tokens
    left_keyval, left_labels = from_behind((own_keyval, labels), "context", 1)
    keys_all = jnp.concatenate([left_keyval, own_keyval], axis=0)
    key_places = jnp.concatenate([left_labels[0], places])
    key_documents = jnp.concatenate([left_labels[1], documents])
    has_left = lax.axis_index("context") > 0
    key_live = jnp.concatenate([jnp.full((tokens,), has_left), jnp.ones((tokens,), dtype=bool)])
    scale_factor = HD ** (-0.5)
    block_rows = 512
    block_starts = jnp.arange(tokens // block_rows) * block_rows

    def block_scores():
        spacing = places[:, None] - key_places[None, :]
        visible = (
            key_live[None, :]
            & (documents[:, None] == key_documents[None, :])
            & (spacing >= 0)
            & (spacing < WINDOW)
        )
        raw_scores = (
            jnp.einsum("qhd,kd->hqk", queries, keys_all[:, :HD], preferred_element_type=jnp.float32)
            * scale_factor
        )
        return (jnp.where(visible[None], raw_scores, -1e30), keys_all, queries)

    def forward_block(start):
        scores, near_keyval, query_block = block_scores()
        row_top = jnp.max(scores, axis=-1, keepdims=True)
        raised = jnp.exp(scores - row_top)
        row_total = jnp.sum(raised, axis=-1, keepdims=True)
        probs = raised / row_total
        mixed_block = jnp.einsum(
            "hqk,kd->qhd",
            probs.astype(jnp.bfloat16),
            near_keyval[:, HD:],
            preferred_element_type=jnp.float32,
        )
        return (mixed_block.astype(jnp.bfloat16), row_top + jnp.log(row_total))

    mixed_blocks, log_blocks = lax.map(forward_block, block_starts)
    mixed_low = mixed_blocks.reshape(tokens, local_heads * HD)
    branch = lax.psum(contract_last(mixed_low, out_all), "tensor")
    post_attn, post_attn_back = jax.vjp(rms_norm, branch, gains_f[1])
    hidden = inputs + post_attn
    normed_mlp_f, pre_mlp_back = jax.vjp(rms_norm, hidden, gains_f[2])
    normed_mlp = normed_mlp_f.astype(jnp.bfloat16)
    columns = normed_mlp
    gate_up = jnp.einsum(
        "bn,nkf->bkf",
        columns,
        lax.all_gather(w_gateup, ("fsdp", "context"), axis=0, tiled=True),
        preferred_element_type=jnp.float32,
    )
    active_f, glu_back = jax.vjp(glu, gate_up)
    active = active_f.astype(jnp.bfloat16)
    down = lax.psum(
        contract_last(
            active, lax.all_gather(w_down, ("fsdp", "context"), axis=0, tiled=True)
        ).astype(jnp.bfloat16),
        "tensor",
    ).astype(jnp.float32)
    post_mlp, post_mlp_back = jax.vjp(rms_norm, down, gains_f[3])
    result = hidden + post_mlp
    grad_out = cotangent[0].astype(jnp.float32)
    d_down, gain_post_mlp = post_mlp_back(grad_out)
    down_low = d_down.astype(jnp.bfloat16)
    columns = down_low
    d_active = jnp.dot(
        columns,
        lax.all_gather(w_down, ("fsdp", "context"), axis=0, tiled=True),
        preferred_element_type=jnp.float32,
    )
    d_gate_up = glu_back(d_active)[0].astype(jnp.bfloat16)
    d_normed_part = jnp.einsum(
        "bkf,nkf->bn",
        d_gate_up,
        lax.all_gather(w_gateup, ("fsdp", "context"), axis=0, tiled=True),
        preferred_element_type=jnp.float32,
    )
    d_normed_mlp = lax.psum(d_normed_part.astype(jnp.bfloat16), "tensor").astype(jnp.float32)
    d_hidden_norm, gain_pre_mlp = pre_mlp_back(d_normed_mlp)
    d_hidden = grad_out + d_hidden_norm
    features = normed_mlp
    grad_cols = down_low
    gate_up_term = jnp.einsum(
        "bn,bkf->nkf", features, d_gate_up, preferred_element_type=jnp.float32
    )
    down_term = contract_first(grad_cols, active)
    mlp_grads = lax.psum_scatter(
        jnp.concatenate([gate_up_term, down_term[:, None, :]], axis=1).astype(jnp.bfloat16),
        ("fsdp", "context"),
        scatter_dimension=0,
        tiled=True,
    ).astype(jnp.float32)
    d_branch, gain_post_attn = post_attn_back(d_hidden)
    branch_low = d_branch.astype(jnp.bfloat16)
    d_mixed = jnp.dot(branch_low, out_all, preferred_element_type=jnp.float32)
    d_mixed_low = d_mixed.astype(jnp.bfloat16).reshape(tokens, local_heads, HD)

    def backward_block(carry, item):
        start, log_block = item
        scores, near_keyval, query_block = block_scores()
        probs_again = jnp.exp(scores - log_block)
        d_probs = jnp.einsum(
            "qhd,kd->hqk", d_mixed_low, near_keyval[:, HD:], preferred_element_type=jnp.float32
        )
        row_inner = jnp.sum(probs_again * d_probs, axis=-1, keepdims=True)
        d_scores = (probs_again * (d_probs - row_inner)).astype(jnp.bfloat16)
        d_query_block = (
            jnp.einsum(
                "hqk,kd->qhd", d_scores, near_keyval[:, :HD], preferred_element_type=jnp.float32
            )
            * scale_factor
        )
        d_keys = (
            jnp.einsum("hqk,qhd->kd", d_scores, query_block, preferred_element_type=jnp.float32)
            * scale_factor
        )
        d_values = jnp.einsum(
            "hqk,qhd->kd",
            probs_again.astype(jnp.bfloat16),
            d_mixed_low,
            preferred_element_type=jnp.float32,
        )
        updated = carry + jnp.concatenate([d_keys, d_values], axis=1)
        return (updated, d_query_block)

    d_keyval, d_query_blocks = lax.scan(
        backward_block,
        jnp.zeros((tokens + tokens, 2 * HD), jnp.float32),
        (block_starts, log_blocks),
    )
    d_queries = d_query_blocks.reshape(tokens, local_heads, HD)
    returned = from_behind(d_keyval[:tokens].astype(jnp.bfloat16), "context", -1).astype(
        jnp.float32
    )
    own_grad = d_keyval[tokens:].at[keep_from:].add(returned)
    d_query_raw, gain_query = query_back(d_queries)
    d_query_low = d_query_raw.reshape(tokens, local_heads * HD).astype(jnp.bfloat16)
    d_normed_query, keyval_grad, gain_query_all = (
        lax.psum(contract_last(d_query_low, query_all).astype(jnp.bfloat16), "tensor").astype(
            jnp.float32
        ),
        lax.psum(own_grad.astype(jnp.bfloat16), "tensor").astype(jnp.float32),
        lax.psum(gain_query.astype(jnp.bfloat16), "tensor").astype(jnp.float32),
    )
    d_key_raw, gain_key = key_back(keyval_grad[:, None, :HD])
    d_keyval_low = jnp.concatenate([d_key_raw[:, 0], keyval_grad[:, HD:]], axis=1).astype(
        jnp.bfloat16
    )
    d_normed = d_normed_query + contract_last(d_keyval_low, keyval_all)
    d_input_norm, gain_input = input_back(d_normed)
    input_total = d_hidden + d_input_norm
    features = normed
    grad_cols = branch_low
    attn_grads = lax.psum_scatter(
        jnp.stack(
            [contract_first(features, d_query_low), contract_first(grad_cols, mixed_low)], axis=1
        ).astype(jnp.bfloat16),
        ("fsdp", "context"),
        scatter_dimension=0,
        tiled=True,
    ).astype(jnp.float32)
    keyval_term = contract_first(normed, d_keyval_low)
    gain_terms = jnp.stack([gain_input, gain_post_attn, gain_pre_mlp, gain_post_mlp])
    head_terms = jnp.stack([gain_query_all, gain_key])
    gain_grad, head_grad, keyval_weight_grad = (
        lax.psum_scatter(
            gain_terms.astype(jnp.bfloat16), ("fsdp", "context"), scatter_dimension=1, tiled=True
        ).astype(jnp.float32),
        lax.psum_scatter(
            head_terms.astype(jnp.bfloat16), ("fsdp", "context"), scatter_dimension=1, tiled=True
        ).astype(jnp.float32),
        lax.psum_scatter(
            keyval_term.astype(jnp.bfloat16), ("fsdp", "context"), scatter_dimension=0, tiled=True
        ).astype(jnp.float32),
    )
    return (
        result[None].astype(jnp.bfloat16),
        input_total[None].astype(jnp.bfloat16),
        gain_grad,
        head_grad,
        attn_grads[:, 0],
        keyval_weight_grad,
        attn_grads[:, 1],
        mlp_grads[:, :2],
        mlp_grads[:, 2],
    )


def solution(mesh):
    return jax.shard_map(
        shards,
        mesh=mesh,
        in_specs=(
            P("fsdp", "context", None),
            P("fsdp", "context"),
            P("fsdp", "context"),
            P(None, ("fsdp", "context")),
            P(None, ("fsdp", "context")),
            P(("fsdp", "context"), "tensor"),
            P(("fsdp", "context"), None),
            P(("fsdp", "context"), "tensor"),
            P(("fsdp", "context"), None, "tensor"),
            P(("fsdp", "context"), "tensor"),
            P("fsdp", "context", None),
        ),
        out_specs=(
            P("fsdp", "context", None),
            P("fsdp", "context", None),
            P(None, ("fsdp", "context")),
            P(None, ("fsdp", "context")),
            P(("fsdp", "context"), "tensor"),
            P(("fsdp", "context"), None),
            P(("fsdp", "context"), "tensor"),
            P(("fsdp", "context"), None, "tensor"),
            P(("fsdp", "context"), "tensor"),
        ),
        check_vma=False,
    )
```

profile of v0, /device:TPU:0, one launch (start us, length us, event | category | flops | bytes accessed | tf_op | source)
XLA Modules:
  0.0 1370.4 jit_solution(6977014308560481948)
XLA Ops:
  8.7 4.9 collective-permute-start.1
  14.3 18.8 %all-gather.1 = bf16[8,32,2]{1,2,0:T(2,128)(2,1)S(1)} all-gather(bf16[1,32,2]{1,2,0:T(2,128)(2,1)} %bitcast.247), channel_id=1, replica_groups=mesh['fsdp'=2,'context'=4,'tensor'=4] {'fsdp','context'}, dimensions={0}, use_global_device_ids=true | all-gather | bytes 1152 | tf_op jit(solution)/shard_map/all_gather | solution.py:73
  33.2 27.2 %all-gather = bf16[8,144,4]{1,2,0:T(4,128)(2,1)S(1)} all-gather(bf16[1,144,4]{1,2,0:T(4,128)(2,1)} %bitcast.246), channel_id=1, replica_groups=mesh['fsdp'=2,'context'=4,'tensor'=4] {'fsdp','context'}, dimensions={0}, use_global_device_ids=true | all-gather | bytes 10368 | tf_op jit(solution)/shard_map/all_gather | solution.py:72
  62.8 32.6 %all_gather.26 = bf16[1152,256]{1,0:T(8,128)(2,1)S(1)} all-gather(bf16[144,256]{1,0:T(8,128)(2,1)} %param.20), channel_id=1, replica_groups=mesh['fsdp'=2,'context'=4,'tensor'=4] {'fsdp','context'}, dimensions={0}, use_global_device_ids=true | all-gather | bytes 663552 | tf_op jit(solution)/shard_map/all_gather | solution.py:74
  105.9 32.7 %all_gather.27 = bf16[1152,256]{1,0:T(8,128)(2,1)S(1)} all-gather(bf16[144,256]{1,0:T(8,128)(2,1)S(1)} %copy-done.37), channel_id=1, replica_groups=mesh['fsdp'=2,'context'=4,'tensor'=4] {'fsdp','context'}, dimensions={0}, use_global_device_ids=true | all-gather | bytes 663552 | tf_op jit(solution)/shard_map/all_gather | solution.py:76
  147.8 55.6 %all-reduce.15.cloned.1.call-done = f32[512,1152]{1,0:T(8,128)} async-done(((f32[512,1152]{1,0:T(8,128)}), f32[512,1152]{1,0:T(8,128)}) %all-reduce.15.cloned.1.call-update) | async-done | bytes 2359312 | tf_op jit(solution)/shard_map/psum | solution.py:136
  208.5 120.5 %all-gather.8.cloned.1.call-done = bf16[1152,2,1728]{2,0,1:T(8,128)(2,1)} async-done(((bf16[144,2,1728]{2,0,1:T(8,128)(2,1)}), bf16[1152,2,1728]{2,0,1:T(8,128)(2,1)}) %all-gather.8.cloned.1.call-update) | async-done | bytes 7962640 | tf_op jit(solution)/shard_map/all_gather | solution.py:145
  329.0 8.3 fusion.110
  337.3 2.9 copy-done.11
  342.7 58.4 %all-gather.10.cloned.1.call-done = bf16[1152,1728]{1,0:T(8,128)(2,1)} async-done(((bf16[144,1728]{1,0:T(8,128)(2,1)}), bf16[1152,1728]{1,0:T(8,128)(2,1)}) %all-gather.10.cloned.1.call-update) | async-done | bytes 3981328 | tf_op jit(solution)/shard_map/all_gather | solution.py:152
  401.1 6.3 convolution_convert_fusion.4
  408.0 35.7 %all-reduce.17.cloned.1.call-done = bf16[512,1152]{1,0:T(8,128)(2,1)} async-done(((bf16[512,1152]{1,0:T(8,128)(2,1)}), bf16[512,1152]{1,0:T(8,128)(2,1)}) %all-reduce.17.cloned.1.call-update) | async-done | bytes 1179664 | tf_op jit(solution)/shard_map/psum | solution.py:150
  445.4 3.4 fusion.36
  448.8 11.4 multiply_bitcast_fusion
  462.0 8.1 fusion.8
  471.6 36.4 %all-reduce.19.cloned.1.call-done = bf16[512,1152]{1,0:T(8,128)(2,1)} async-done(((bf16[512,1152]{1,0:T(8,128)(2,1)}), bf16[512,1152]{1,0:T(8,128)(2,1)}) %all-reduce.19.cloned.1.call-update) | async-done | bytes 1179664 | tf_op jit(solution)/shard_map/psum | solution.py:174
  508.0 3.5 fusion.27
  511.6 4.5 multiply_reduce_fusion
  527.6 11.5 collective-permute-done.2
  544.1 7.0 psum.47
  556.0 28.6 %all-reduce.23.cloned.1.call-done = (bf16[512,1152]{1,0:T(8,128)(2,1)}, bf16[512,512]{0,1:T(8,128)(2,1)}) async-done(((bf16[512,1152]{1,0:T(8,128)(2,1)}, bf16[512,512]{0,1:T(8,128)(2,1)}), (bf16[512,1152]{1,0:T(8,128)(2,1)}, bf16[512,512]{0,1:T(8,128)(2,1)})) %all-reduce.23.cloned.1.call-update) | async-done | bytes 1703952 | tf_op jit(solution)/shard_map/psum | solution.py:235
  587.5 3.3 fusion.25
  597.9 3.1 convolution_convert_fusion.2
  601.1 6.6 fusion
  607.7 9.4 convolution_convert_fusion
  617.1 7.5 pad_maximum_fusion
  624.5 27.1 %copy.35 = bf16[1152,3,1728]{2,1,0:T(4,128)(2,1)} copy(bf16[1152,3,1728]{0,2,1:T(8,128)(2,1)} %pad_maximum_fusion) | data formatting | bytes 23887872 | tf_op jit(solution)/shard_map/concatenate | solution.py:184
  654.5 3.3 fusion.48
  659.1 59.0 %reduce-scatter.13.cloned.1.call-done = bf16[144,4]{1,0:T(8,128)(2,1)} async-done(((bf16[1152,4]{1,0:T(8,128)(2,1)}), bf16[144,4]{1,0:T(8,128)(2,1)}) %reduce-scatter.13.cloned.1.call-update) | async-done | bytes 1168
  719.6 65.5 %reduce-scatter.9.cloned.1.call-done = bf16[144,2,256]{2,0,1:T(8,128)(2,1)} async-done(((bf16[1152,2,256]{2,0,1:T(8,128)(2,1)}), bf16[144,2,256]{2,0,1:T(8,128)(2,1)}) %reduce-scatter.9.cloned.1.call-update) | async-done | bytes 147472 | tf_op jit(solution)/shard_map/reduce_scatter | solution.py:250
  786.7 65.4 %reduce-scatter.11.cloned.1.call-done = bf16[144,512]{1,0:T(8,128)(2,1)} async-done(((bf16[1152,512]{1,0:T(8,128)(2,1)}), bf16[144,512]{1,0:T(8,128)(2,1)}) %reduce-scatter.11.cloned.1.call-update) | async-done | bytes 147472 | tf_op jit(solution)/shard_map/reduce_scatter | solution.py:268
  853.7 503.4 %all-reduce.21.cloned.1.call-done = bf16[1152,3,1728]{2,1,0:T(4,128)(2,1)} async-done(((bf16[1152,3,1728]{2,1,0:T(4,128)(2,1)}), bf16[1152,3,1728]{2,1,0:T(4,128)(2,1)}) %all-reduce.21.cloned.1.call-update) | async-done | bytes 11943952
  (294 shorter events, 82.4 us)
Async XLA Ops:
  7.2 92.0 %all-gather.6.cloned.1.call-start = ((), (), s32[]{:S(2)}) async-start(), calls=%async_computation.4 | async-start | bytes 1327104 | tf_op jit(solution)/shard_map/all_gather | solution.py:75
  7.9 195.5 %all-reduce.15.cloned.1.call-start = ((), (), s32[]{:S(2)}) async-start(), calls=%async_computation.5 | async-start | bytes 4718592 | tf_op jit(solution)/shard_map/psum | solution.py:136
  8.7 130.0 %collective-permute-start.1 = (s32[2,512]{1,0:T(2,128)S(1)}, s32[2,512]{1,0:T(2,128)S(1)}, u32[]{:S(2)}, u32[]{:S(2)}) collective-permute-start(s32[2,512]{1,0:T(2,128)S(1)} %pad_add_fusion.2), channel_id=1, source_target_pairs={{0,4},{4,8},{8,12},{1,5},{5,9},{9,13},{2,6},{6,10},{10,14},{3,7},{... | collective-permute-start | bytes 12296 | tf_op jit(solution)/shard_map/ppermute | solution.py:14
  14.3 87.5 %copy-start.41 = (f32[512]{0:T(512)}, f32[512]{0:T(512)S(1)}, u32[]{:S(2)}) copy-start(f32[512]{0:T(512)S(1)} %convert_element_type.160) | copy-start | bytes 6148
  60.5 41.3 %copy-start.78 = (f32[128]{0:T(128)}, f32[128]{0:T(128)S(1)}, u32[]{:S(2)}) copy-start(f32[128]{0:T(128)S(1)} %multiply_power_fusion) | copy-start | bytes 1540
  61.1 38.1 %copy-start.47 = (f32[1152]{0:T(1024)}, f32[1152]{0:T(1024)S(1)}, u32[]{:S(2)}) copy-start(f32[1152]{0:T(1024)S(1)} %get-tuple-element.128) | copy-start | bytes 13828
  62.7 35.5 %copy-start.57 = (f32[512]{0:T(512)}, f32[512]{0:T(512)S(1)}, u32[]{:S(2)}) copy-start(f32[512]{0:T(512)S(1)} %fusion.28) | copy-start | bytes 6148
  62.7 36.5 %copy-start.75 = (f32[512]{0:T(512)}, f32[512]{0:T(512)S(1)}, u32[]{:S(2)}) copy-start(f32[512]{0:T(512)S(1)} %fusion.112) | copy-start | bytes 6148
  62.7 36.4 %copy-start.68 = (f32[1,256]{1,0:T(1,128)}, f32[1,256]{1,0:T(1,128)S(1)}, u32[]{:S(2)}) copy-start(f32[1,256]{1,0:T(1,128)S(1)} %get-tuple-element.153) | copy-start | bytes 3076
  62.7 38.9 %copy-start.66 = (f32[1,256]{1,0:T(1,128)}, f32[1,256]{1,0:T(1,128)S(1)}, u32[]{:S(2)}) copy-start(f32[1,256]{1,0:T(1,128)S(1)} %get-tuple-element.154) | copy-start | bytes 3076
  62.8 36.5 %copy-start.8 = (bf16[1,512,1152]{2,1,0:T(8,128)(2,1)S(1)}, bf16[1,512,1152]{2,1,0:T(8,128)(2,1)}, u32[]{:S(2)}) copy-start(bf16[1,512,1152]{2,1,0:T(8,128)(2,1)} %param.15) | copy-start | bytes 3538948
  101.7 37.0 %copy-start.43 = (f32[512]{0:T(512)}, f32[512]{0:T(512)S(1)}, u32[]{:S(2)}) copy-start(f32[512]{0:T(512)S(1)} %fusion.113) | copy-start | bytes 6148
  101.7 37.0 %copy-start.62 = (s32[1,512]{1,0:T(1,128)S(1)}, s32[1,512]{1,0:T(1,128)}, u32[]{:S(2)}) copy-start(s32[1,512]{1,0:T(1,128)} %param.16) | copy-start | bytes 6148
  101.7 37.0 %copy-start.72 = (s32[1,512]{1,0:T(1,128)S(1)}, s32[1,512]{1,0:T(1,128)}, u32[]{:S(2)}) copy-start(s32[1,512]{1,0:T(1,128)} %param.17) | copy-start | bytes 6148
  103.7 38.6 %copy-start.30 = (bf16[512,128]{0,1:T(8,128)(2,1)}, bf16[512,128]{0,1:T(8,128)(2,1)S(1)}, u32[]{:S(2)}) copy-start(bf16[512,128]{0,1:T(8,128)(2,1)S(1)} %get-tuple-element.141) | copy-start | bytes 393220
  103.8 34.9 %collective-permute-start = (bf16[512,512]{0,1:T(8,128)(2,1)S(1)}, bf16[512,512]{0,1:T(8,128)(2,1)}, u32[]{:S(2)}, u32[]{:S(2)}) collective-permute-start(bf16[512,512]{0,1:T(8,128)(2,1)S(1)} %pad_maximum_fusion.3), channel_id=1, source_target_pairs={{0,4},{4,8},{8,12},{1,5},{5,9},{9,13},{2,6},{6,10},{10,14},{3,7},{... | collective-permute-start | bytes 1572872 | tf_op jit(solution)/shard_map/ppermute | solution.py:14
  145.7 183.3 %all-gather.8.cloned.1.call-start = ((), (), s32[]{:S(2)}) async-start(), calls=%async_computation.6 | async-start | bytes 9289728 | tf_op jit(solution)/shard_map/all_gather | solution.py:145
  146.9 254.2 %all-gather.10.cloned.1.call-start = ((), (), s32[]{:S(2)}) async-start(), calls=%async_computation.7 | async-start | bytes 4644864 | tf_op jit(solution)/shard_map/all_gather | solution.py:152
  147.5 296.3 %all-reduce.17.cloned.1.call-start = ((), (), s32[]{:S(2)}) async-start(), calls=%async_computation.8 | async-start | bytes 2359296 | tf_op jit(solution)/shard_map/psum | solution.py:150
  208.5 128.8 %copy-start.50 = (f32[512]{0:T(512)}, f32[512]{0:T(512)S(1)}, u32[]{:S(2)}) copy-start(f32[512]{0:T(512)S(1)} %fusion.116) | copy-start | bytes 6148
  407.4 100.6 %all-reduce.19.cloned.1.call-start = ((), (), s32[]{:S(2)}) async-start(), calls=%async_computation.9 | async-start | bytes 2359296 | tf_op jit(solution)/shard_map/psum | solution.py:174
  470.1 114.4 %all-reduce.23.cloned.1.call-start = ((), (), s32[]{:S(2)}) async-start(), calls=%async_computation.15 | async-start | bytes 3407872 | tf_op jit(solution)/shard_map/psum | solution.py:235
  523.7 15.5 %collective-permute-start.2 = (bf16[512,512]{0,1:T(8,128)(2,1)S(1)}, bf16[512,512]{0,1:T(8,128)(2,1)S(1)}, u32[]{:S(2)}, u32[]{:S(2)}) collective-permute-start(bf16[512,512]{0,1:T(8,128)(2,1)S(1)} %fusion.62), channel_id=1, source_target_pairs={{4,0},{8,4},{12,8},{5,1},{9,5},{13,9},{6,2},{10,6},{14,10},{7,3},{... | collective-permute-start | bytes 1572872 | tf_op jit(solution)/shard_map/ppermute | solution.py:14
  540.2 117.6 %reduce-scatter.15.cloned.1.call-start = ((), (), s32[]{:S(2)}) async-start(), calls=%async_computation.13 | async-start | bytes 73728
  553.4 32.4 %copy-start.80 = (f32[128]{0:T(128)S(1)}, f32[128]{0:T(128)}, u32[]{:S(2)}) copy-start(f32[128]{0:T(128)} %copy-done.78) | copy-start | bytes 1540
  553.4 33.6 %copy-start.13 = (f32[512,512]{0,1:T(8,128)S(1)}, f32[512,512]{0,1:T(8,128)}, u32[]{:S(2)}) copy-start(f32[512,512]{0,1:T(8,128)} %copy-done.12) | copy-start | bytes 3145732
  553.4 33.6 %copy-start.44 = (f32[512]{0:T(512)S(1)}, f32[512]{0:T(512)}, u32[]{:S(2)}) copy-start(f32[512]{0:T(512)} %copy-done.43) | copy-start | bytes 6148
  553.4 33.6 %copy-start.67 = (f32[1,256]{1,0:T(1,128)S(1)}, f32[1,256]{1,0:T(1,128)}, u32[]{:S(2)}) copy-start(f32[1,256]{1,0:T(1,128)} %copy-done.66) | copy-start | bytes 3076
  593.4 124.7 %reduce-scatter.13.cloned.1.call-start = ((), (), s32[]{:S(2)}) async-start(), calls=%async_computation.12 | async-start | bytes 331776
  596.4 188.6 %reduce-scatter.9.cloned.1.call-start = ((), (), s32[]{:S(2)}) async-start(), calls=%async_computation.10 | async-start | bytes 1327104 | tf_op jit(solution)/shard_map/reduce_scatter | solution.py:250
  597.7 254.4 %reduce-scatter.11.cloned.1.call-start = ((), (), s32[]{:S(2)}) async-start(), calls=%async_computation.11 | async-start | bytes 1327104 | tf_op jit(solution)/shard_map/reduce_scatter | solution.py:268
  601.0 756.1 %all-reduce.21.cloned.1.call-start = ((), (), s32[]{:S(2)}) async-start(), calls=%async_computation.14 | async-start | bytes 33030144
  (71 other events, 334.5 us)
Sparse Core Ops, SparseCore 0:
  10.1 43.7 all-gather.5
  145.8 57.4 all-reduce.14
  206.1 122.8 all-gather.7
  331.0 70.0 all-gather.9
  407.6 36.1 all-reduce.16
  470.2 37.7 all-reduce.18
  540.3 44.1 all-reduce.22
  593.5 62.4 reduce-scatter.14
  659.9 58.1 reduce-scatter.12
  721.3 63.6 reduce-scatter.8
  788.4 63.5 reduce-scatter.10
  856.0 501.0 all-reduce.20
where the time goes:
time: 1380 us; the launch traced here: 1370 us
  waiting for transfers between devices  1040 us (75%)
  blocking collectives  118 us (9%)
  matrix products  74.4 us (5%)
  other arithmetic  55 us (4%)
  local copies, waits for them, and re-layouts  54.9 us (4%)
  between operations  16.3 us (1%)
    unnamed x15, waiting for transfers between devices  564 us
    all_gather x1, waiting for transfers between devices, shards(): lax.all_gather(w_gateup, ('fsdp', 'context'), axis=0, tiled=True)  121 us
    reduce_scatter x1, waiting for transfers between devices, shards(): lax.psum_scatter(jnp.stack([contract_first(features, d_query_low), contra...  65.5 us
    reduce_scatter x1, waiting for transfers between devices, shards(): lax.psum_scatter(keyval_term.astype(jnp.bfloat16), ('fsdp', 'context'), s...  65.4 us
    all_gather x1, waiting for transfers between devices, shards(): lax.all_gather(w_down, ('fsdp', 'context'), axis=0, tiled=True)  58.4 us
    psum x1, waiting for transfers between devices, shards(): branch = lax.psum(contract_last(mixed_low, out_all), 'tensor')  55.6 us
    psum x1, waiting for transfers between devices, shards(): lax.psum(d_normed_part.astype(jnp.bfloat16), 'tensor').astype(jnp.float32)  36.4 us
    psum x1, waiting for transfers between devices, shards(): lax.psum(contract_last(active, lax.all_gather(w_down, ('fsdp', 'context')...  35.7 us
  transfers between devices with their start and end apart: 15, of which 11 were waited for; matrix products, arithmetic and copies ran while one was open for 8% of the time, Pallas kernels for 0%

commit v1 on v0

--- a/solution.py
+++ b/solution.py
@@ -6,6 +6,22 @@
 HD = 256
 WINDOW = 512
 EPSILON = 1e-06
+
+
+def summed_both_ways(shard, axis, dim, product):
+    devices, index, span = (lax.axis_size(axis), lax.axis_index(axis), shard.shape[dim])
+    right = [(i, (i + 1) % devices) for i in range(devices)]
+    left = [(i, (i - 1) % devices) for i in range(devices)]
+    halfway = devices // 2
+    from_left = from_right = shard
+    running = product(shard, index * span)
+    for hop in range(1, halfway + 1):
+        from_left = lax.ppermute(from_left, axis, right)
+        if hop < devices - halfway:
+            from_right = lax.ppermute(from_right, axis, left)
+            running = running + product(from_right, (index + hop) % devices * span)
+        running = running + product(from_left, (index - hop) % devices * span)
+    return running
 
 
 def from_behind(block, axis, distance):
@@ -139,11 +155,16 @@
     normed_mlp_f, pre_mlp_back = jax.vjp(rms_norm, hidden, gains_f[2])
     normed_mlp = normed_mlp_f.astype(jnp.bfloat16)
     columns = normed_mlp
-    gate_up = jnp.einsum(
-        "bn,nkf->bkf",
-        columns,
-        lax.all_gather(w_gateup, ("fsdp", "context"), axis=0, tiled=True),
-        preferred_element_type=jnp.float32,
+    gate_up = summed_both_ways(
+        w_gateup,
+        ("fsdp", "context"),
+        0,
+        lambda shard, offset: jnp.einsum(
+            "bn,nkf->bkf",
+            lax.dynamic_slice_in_dim(columns, offset, shard.shape[0], axis=1),
+            shard,
+            preferred_element_type=jnp.float32,
+        ),
     )
     active_f, glu_back = jax.vjp(glu, gate_up)
     active = active_f.astype(jnp.bfloat16)

time: 1380 us -> 1440 us (1.043)
  waiting for transfers between devices: 1040 us -> 974 us
  blocking collectives: 118 us -> 174 us
  matrix products: 74.4 us -> 125 us
  starting transfers between devices: 10.2 us -> 38.4 us
    psum x1, waiting for transfers between devices: 55.6 us -> 0.02 us  [shards(): branch = lax.psum(contract_last(mixed_low, out_all), 'tensor')]
    all_gather x1, waiting for transfers between devices: 58.4 us -> 7.28 us  [shards(): lax.all_gather(w_down, ('fsdp', 'context'), axis=0, tiled=True)]
    all_gather x1, blocking collectives: 27.2 us -> 76.2 us  [shards(): lax.all_gather(norm_gains, ('fsdp', 'context'), axis=1, tiled=True)]
    dot_general x1 -> x8, matrix products: 8.27 us -> 56.9 us  [shards(): jnp.einsum('bn,nkf->bkf', lax.dynamic_slice_in_dim(columns, offset, shard...]
    ppermute x0 -> x7, waiting for transfers between devices: none -> 39.2 us  [the longest x4 35.2 us: summed_both_ways(): from_left = lax.ppermute(from_left, axis, right)]
    ppermute x0 -> x7, starting transfers between devices: none -> 32.3 us  [the longest x4 21.3 us: summed_both_ways(): from_left = lax.ppermute(from_left, axis, right)]
  transfers between devices with their start and end apart: 15 -> 22, of which waited for: 11 -> 14; matrix products, arithmetic and copies ran while one was open for 8% -> 13% of each run, Pallas kernels for 0% -> 0%
where the time goes in v1:
time: 1440 us; the launch traced here: 1430 us
  waiting for transfers between devices  974 us (68%)
  blocking collectives  174 us (12%)
  matrix products  125 us (9%)
  other arithmetic  55 us (4%)
  local copies, waits for them, and re-layouts  50.4 us (4%)
  starting transfers between devices  38.4 us (3%)
  between operations  16.4 us (1%)
    unnamed x15, waiting for transfers between devices  565 us
    all_gather x1, waiting for transfers between devices, shards(): lax.all_gather(w_gateup, ('fsdp', 'context'), axis=0, tiled=True)  108 us
    all_gather x1, blocking collectives, shards(): lax.all_gather(norm_gains, ('fsdp', 'context'), axis=1, tiled=True)  76.2 us
    reduce_scatter x1, waiting for transfers between devices, shards(): lax.psum_scatter(jnp.stack([contract_first(features, d_query_low), contra...  65.4 us
    reduce_scatter x1, waiting for transfers between devices, shards(): lax.psum_scatter(keyval_term.astype(jnp.bfloat16), ('fsdp', 'context'), s...  65.3 us
    dot_general x8, matrix products, shards(): jnp.einsum('bn,nkf->bkf', lax.dynamic_slice_in_dim(columns, offset, shard...  56.9 us
    psum x1, waiting for transfers between devices, shards(): lax.psum(contract_last(active, lax.all_gather(w_down, ('fsdp', 'context')...  50 us
    all_gather x1, blocking collectives, shards(): lax.all_gather(w_out, ('fsdp', 'context'), axis=0, tiled=True)  39.7 us
  transfers between devices with their start and end apart: 22, of which 14 were waited for; matrix products, arithmetic and copies ran while one was open for 13% of the time, Pallas kernels for 0%

profile of v1, /device:TPU:0, one launch (start us, length us, event | category | flops | bytes accessed | tf_op | source)
XLA Modules:
  0.0 1432.6 jit_solution(10466160254566446963)
XLA Ops:
  8.7 6.1 collective-permute-start.2
  18.0 76.2 %all-gather = bf16[8,144,4]{1,2,0:T(4,128)(2,1)S(1)} all-gather(bf16[1,144,4]{1,2,0:T(4,128)(2,1)} %bitcast.275), channel_id=1, replica_groups=mesh['fsdp'=2,'context'=4,'tensor'=4] {'fsdp','context'}, dimensions={0}, use_global_device_ids=true | all-gather | bytes 10368 | tf_op jit(solution)/shard_map/all_gather | solution.py:88
  94.3 18.4 %all-gather.1 = bf16[8,32,2]{1,2,0:T(2,128)(2,1)S(1)} all-gather(bf16[1,32,2]{1,2,0:T(2,128)(2,1)} %bitcast.276), channel_id=1, replica_groups=mesh['fsdp'=2,'context'=4,'tensor'=4] {'fsdp','context'}, dimensions={0}, use_global_device_ids=true | all-gather | bytes 1152 | tf_op jit(solution)/shard_map/all_gather | solution.py:89
  113.8 32.4 %all_gather.25 = bf16[1152,256]{1,0:T(8,128)(2,1)S(1)} all-gather(bf16[144,256]{1,0:T(8,128)(2,1)S(1)} %copy-done.39), channel_id=1, replica_groups=mesh['fsdp'=2,'context'=4,'tensor'=4] {'fsdp','context'}, dimensions={0}, use_global_device_ids=true | all-gather | bytes 663552 | tf_op jit(solution)/shard_map/all_gather | solution.py:90
  156.1 39.7 %all_gather.26 = bf16[1152,256]{1,0:T(8,128)(2,1)S(1)} all-gather(bf16[144,256]{1,0:T(8,128)(2,1)S(1)} %copy-done.40), channel_id=1, replica_groups=mesh['fsdp'=2,'context'=4,'tensor'=4] {'fsdp','context'}, dimensions={0}, use_global_device_ids=true | all-gather | bytes 663552 | tf_op jit(solution)/shard_map/all_gather | solution.py:92
  210.5 17.0 %collective-permute-done.5 = bf16[144,2,1728]{2,0,1:T(8,128)(2,1)} collective-permute-done((bf16[144,2,1728]{2,0,1:T(8,128)(2,1)}, bf16[144,2,1728]{2,0,1:T(8,128)(2,1)}, u32[]{:S(2)}, u32[]{:S(2)}) %collective-permute-start.5) | collective-permute-done | bytes 995360 | tf_op jit(solution)/shard_map/ppermute | solution.py:19
  227.5 17.7 %collective-permute-start.7 = (bf16[144,2,1728]{2,0,1:T(8,128)(2,1)}, bf16[144,2,1728]{2,0,1:T(8,128)(2,1)}, u32[]{:S(2)}, u32[]{:S(2)}) collective-permute-start(bf16[144,2,1728]{2,0,1:T(8,128)(2,1)} %collective-permute-done.5), channel_id=1, source_target_pairs={{0,4},{4,8},{8,12},{12,16},{16,20},{20,24},{24,28},{28,0},{1,5},{5... | collective-permute-start | bytes 2985992 | tf_op jit(solution)/shard_map/ppermute | solution.py:19
  251.5 18.2 %collective-permute-done.7 = bf16[144,2,1728]{2,0,1:T(8,128)(2,1)} collective-permute-done((bf16[144,2,1728]{2,0,1:T(8,128)(2,1)}, bf16[144,2,1728]{2,0,1:T(8,128)(2,1)}, u32[]{:S(2)}, u32[]{:S(2)}) %collective-permute-start.7) | collective-permute-done | bytes 995360 | tf_op jit(solution)/shard_map/ppermute | solution.py:19
  279.5 5.3 fusion.111
  284.9 5.3 fusion.113
  290.2 5.4 fusion.115
  295.6 5.4 fusion.117
  300.9 5.3 fusion.107
  306.2 5.6 fusion.109
  311.8 20.5 %add_add_fusion = f32[512,2,1728]{0,2,1:T(8,128)} fusion(f32[512,2,1728]{0,2,1:T(8,128)} %fusion.107, f32[512,2,1728]{0,2,1:T(8,128)} %fusion.109, f32[512,2,1728]{0,2,1:T(8,128)} %fusion.111, f32[512,2,1728]{0,2,1:T(8,128)} %fusion.113, f32[512,2,1728]{0,2,1:T(8,128)} %fusion.115, f32[512,2,1728]{0,2,1:T(8,128)} %fusion.119, f32[512,2,1728]{0,2,1:T(8,128)} %fusion.117, ...), kind=kOutput, calls=%fused_computation.4 | convolution fusion | flops 521994240 | bytes 57880580 | tf_op jit(solution)/shard_map/bn,nkf->bkf/dot_general | solution.py:162
  332.2 5.6 multiply_convert_fusion
  337.8 7.3 all-gather.8.cloned.1.call-done
  345.1 6.3 convolution_convert_fusion.4
  352.1 50.0 %all-reduce.17.cloned.1.call-done = bf16[512,1152]{1,0:T(8,128)(2,1)} async-done(((bf16[512,1152]{1,0:T(8,128)(2,1)}), bf16[512,1152]{1,0:T(8,128)(2,1)}) %all-reduce.17.cloned.1.call-update) | async-done | bytes 1179664 | tf_op jit(solution)/shard_map/psum | solution.py:171
  407.6 12.1 multiply_bitcast_fusion
  419.7 108.0 %all-gather.10.cloned.1.call-done = bf16[1152,2,1728]{2,0,1:T(8,128)(2,1)} async-done(((bf16[144,2,1728]{2,0,1:T(8,128)(2,1)}), bf16[1152,2,1728]{2,0,1:T(8,128)(2,1)}) %all-gather.10.cloned.1.call-update) | async-done | bytes 7962640 | tf_op jit(solution)/shard_map/all_gather | solution.py:192
  527.7 11.4 fusion.8
  540.4 34.5 %all-reduce.19.cloned.1.call-done = bf16[512,1152]{1,0:T(8,128)(2,1)} async-done(((bf16[512,1152]{1,0:T(8,128)(2,1)}), bf16[512,1152]{1,0:T(8,128)(2,1)}) %all-reduce.19.cloned.1.call-update) | async-done | bytes 1179664 | tf_op jit(solution)/shard_map/psum | solution.py:195
  595.1 10.4 collective-permute-done.9
  610.3 7.0 psum.47
  622.1 28.7 %all-reduce.23.cloned.1.call-done = (bf16[512,1152]{1,0:T(8,128)(2,1)}, bf16[512,512]{0,1:T(8,128)(2,1)}) async-done(((bf16[512,1152]{1,0:T(8,128)(2,1)}, bf16[512,512]{0,1:T(8,128)(2,1)}), (bf16[512,1152]{1,0:T(8,128)(2,1)}, bf16[512,512]{0,1:T(8,128)(2,1)})) %all-reduce.23.cloned.1.call-update) | async-done | bytes 1703952 | tf_op jit(solution)/shard_map/psum | solution.py:256
  670.9 9.1 convolution_convert_fusion
  685.3 27.0 %copy.79 = bf16[1152,3,1728]{2,1,0:T(4,128)(2,1)} copy(bf16[1152,3,1728]{0,2,1:T(8,128)(2,1)} %pad_maximum_fusion) | data formatting | bytes 23887872 | tf_op jit(solution)/shard_map/concatenate | solution.py:205
  719.7 60.7 %reduce-scatter.13.cloned.1.call-done = bf16[144,4]{1,0:T(8,128)(2,1)} async-done(((bf16[1152,4]{1,0:T(8,128)(2,1)}), bf16[144,4]{1,0:T(8,128)(2,1)}) %reduce-scatter.13.cloned.1.call-update) | async-done | bytes 1168
  781.9 65.4 %reduce-scatter.9.cloned.1.call-done = bf16[144,2,256]{2,0,1:T(8,128)(2,1)} async-done(((bf16[1152,2,256]{2,0,1:T(8,128)(2,1)}), bf16[144,2,256]{2,0,1:T(8,128)(2,1)}) %reduce-scatter.9.cloned.1.call-update) | async-done | bytes 147472 | tf_op jit(solution)/shard_map/reduce_scatter | solution.py:271
  849.0 65.3 %reduce-scatter.11.cloned.1.call-done = bf16[144,512]{1,0:T(8,128)(2,1)} async-done(((bf16[1152,512]{1,0:T(8,128)(2,1)}), bf16[144,512]{1,0:T(8,128)(2,1)}) %reduce-scatter.11.cloned.1.call-update) | async-done | bytes 147472 | tf_op jit(solution)/shard_map/reduce_scatter | solution.py:289
  915.9 503.4 %all-reduce.21.cloned.1.call-done = bf16[1152,3,1728]{2,1,0:T(4,128)(2,1)} async-done(((bf16[1152,3,1728]{2,1,0:T(4,128)(2,1)}), bf16[1152,3,1728]{2,1,0:T(4,128)(2,1)}) %all-reduce.21.cloned.1.call-update) | async-done | bytes 11943952
  (313 shorter events, 125.8 us)
Async XLA Ops:
  7.2 105.6 %copy-start.66 = (s32[1,512]{1,0:T(1,128)S(1)}, s32[1,512]{1,0:T(1,128)}, u32[]{:S(2)}) copy-start(s32[1,512]{1,0:T(1,128)} %param.16) | copy-start | bytes 6148
  7.2 106.2 %copy-start.8 = (bf16[1,512,1152]{2,1,0:T(8,128)(2,1)S(1)}, bf16[1,512,1152]{2,1,0:T(8,128)(2,1)}, u32[]{:S(2)}) copy-start(bf16[1,512,1152]{2,1,0:T(8,128)(2,1)} %param.15) | copy-start | bytes 3538948
  7.2 106.6 %copy-start.39 = (bf16[144,256]{1,0:T(8,128)(2,1)S(1)}, bf16[144,256]{1,0:T(8,128)(2,1)}, u32[]{:S(2)}) copy-start(bf16[144,256]{1,0:T(8,128)(2,1)} %param.20) | copy-start | bytes 221188
  7.2 141.4 %all-gather.6.cloned.1.call-start = ((), (), s32[]{:S(2)}) async-start(), calls=%async_computation.4 | async-start | bytes 1327104 | tf_op jit(solution)/shard_map/all_gather | solution.py:91
  8.7 138.2 %copy-start.22 = (bf16[144,2,1728]{2,0,1:T(8,128)(2,1)}, bf16[144,2,1728]{2,0,1:T(8,128)(2,1)S(1)}, u32[]{:S(2)}) copy-start(bf16[144,2,1728]{2,0,1:T(8,128)(2,1)S(1)} %copy.68) | copy-start | bytes 2985988
  8.7 198.9 %collective-permute-start.2 = (bf16[144,2,1728]{2,0,1:T(8,128)(2,1)S(1)}, bf16[144,2,1728]{2,0,1:T(8,128)(2,1)}, u32[]{:S(2)}, u32[]{:S(2)}) collective-permute-start(bf16[144,2,1728]{2,0,1:T(8,128)(2,1)S(1)} %copy.68), channel_id=1, source_target_pairs={{0,28},{4,0},{8,4},{12,8},{16,12},{20,16},{24,20},{28,24},{1,29},{... | collective-permute-start | bytes 2985992 | tf_op jit(solution)/shard_map/ppermute | solution.py:21
  14.7 182.5 %collective-permute-start.3 = (bf16[144,2,1728]{2,0,1:T(8,128)(2,1)S(1)}, bf16[144,2,1728]{2,0,1:T(8,128)(2,1)}, u32[]{:S(2)}, u32[]{:S(2)}) collective-permute-start(bf16[144,2,1728]{2,0,1:T(8,128)(2,1)S(1)} %copy.68), channel_id=1, source_target_pairs={{0,4},{4,8},{8,12},{12,16},{16,20},{20,24},{24,28},{28,0},{1,5},{5... | collective-permute-start | bytes 2985992 | tf_op jit(solution)/shard_map/ppermute | solution.py:19
  14.8 255.1 %all-reduce.15.cloned.1.call-start = ((), (), s32[]{:S(2)}) async-start(), calls=%async_computation.5 | async-start | bytes 4718592 | tf_op jit(solution)/shard_map/psum | solution.py:152
  16.1 179.7 %collective-permute-start.1 = (s32[2,512]{1,0:T(2,128)}, s32[2,512]{1,0:T(2,128)}, u32[]{:S(2)}, u32[]{:S(2)}) collective-permute-start(s32[2,512]{1,0:T(2,128)} %pad_add_fusion.2), channel_id=1, source_target_pairs={{0,4},{4,8},{8,12},{1,5},{5,9},{9,13},{2,6},{6,10},{10,14},{3,7},{... | collective-permute-start | bytes 12296 | tf_op jit(solution)/shard_map/ppermute | solution.py:30
  112.8 38.5 %copy-start.46 = (f32[512]{0:T(512)}, f32[512]{0:T(512)S(1)}, u32[]{:S(2)}) copy-start(f32[512]{0:T(512)S(1)} %convert_element_type.160) | copy-start | bytes 6148
  112.8 38.5 %copy-start.81 = (f32[128]{0:T(128)}, f32[128]{0:T(128)S(1)}, u32[]{:S(2)}) copy-start(f32[128]{0:T(128)S(1)} %multiply_power_fusion) | copy-start | bytes 1540
  113.8 37.3 %copy-start.71 = (f32[1,256]{1,0:T(1,128)}, f32[1,256]{1,0:T(1,128)S(1)}, u32[]{:S(2)}) copy-start(f32[1,256]{1,0:T(1,128)S(1)} %get-tuple-element.154) | copy-start | bytes 3076
  151.1 44.6 %copy-start.48 = (f32[512]{0:T(512)}, f32[512]{0:T(512)S(1)}, u32[]{:S(2)}) copy-start(f32[512]{0:T(512)S(1)} %fusion.141) | copy-start | bytes 6148
  153.2 51.0 %copy-start.34 = (bf16[512,128]{0,1:T(8,128)(2,1)}, bf16[512,128]{0,1:T(8,128)(2,1)S(1)}, u32[]{:S(2)}) copy-start(bf16[512,128]{0,1:T(8,128)(2,1)S(1)} %get-tuple-element.141) | copy-start | bytes 393220
  153.2 48.7 %copy-start.67 = (s32[1,512]{1,0:T(1,128)S(1)}, s32[1,512]{1,0:T(1,128)}, u32[]{:S(2)}) copy-start(s32[1,512]{1,0:T(1,128)} %param.16) | copy-start | bytes 6148
  154.0 46.7 %collective-permute-start = (bf16[512,512]{0,1:T(8,128)(2,1)}, bf16[512,512]{0,1:T(8,128)(2,1)}, u32[]{:S(2)}, u32[]{:S(2)}) collective-permute-start(bf16[512,512]{0,1:T(8,128)(2,1)} %pad_maximum_fusion.3), channel_id=1, source_target_pairs={{0,4},{4,8},{8,12},{1,5},{5,9},{9,13},{2,6},{6,10},{10,14},{3,7},{... | collective-permute-start | bytes 1572872 | tf_op jit(solution)/shard_map/ppermute | solution.py:30
  197.3 30.2 %collective-permute-start.5 = (bf16[144,2,1728]{2,0,1:T(8,128)(2,1)}, bf16[144,2,1728]{2,0,1:T(8,128)(2,1)}, u32[]{:S(2)}, u32[]{:S(2)}) collective-permute-start(bf16[144,2,1728]{2,0,1:T(8,128)(2,1)} %collective-permute-done.3), channel_id=1, source_target_pairs={{0,4},{4,8},{8,12},{12,16},{16,20},{20,24},{24,28},{28,0},{1,5},{5... | collective-permute-start | bytes 2985992 | tf_op jit(solution)/shard_map/ppermute | solution.py:19
  207.6 137.5 %all-gather.8.cloned.1.call-start = ((), (), s32[]{:S(2)}) async-start(), calls=%async_computation.6 | async-start | bytes 4644864 | tf_op jit(solution)/shard_map/all_gather | solution.py:173
  207.6 41.8 %collective-permute-start.4 = (bf16[144,2,1728]{2,0,1:T(8,128)(2,1)}, bf16[144,2,1728]{2,0,1:T(8,128)(2,1)}, u32[]{:S(2)}, u32[]{:S(2)}) collective-permute-start(bf16[144,2,1728]{2,0,1:T(8,128)(2,1)} %collective-permute-done.2), channel_id=1, source_target_pairs={{0,28},{4,0},{8,4},{12,8},{16,12},{20,16},{24,20},{28,24},{1,29},{... | collective-permute-start | bytes 2985992 | tf_op jit(solution)/shard_map/ppermute | solution.py:21
  227.5 42.2 %collective-permute-start.7 = (bf16[144,2,1728]{2,0,1:T(8,128)(2,1)}, bf16[144,2,1728]{2,0,1:T(8,128)(2,1)}, u32[]{:S(2)}, u32[]{:S(2)}) collective-permute-start(bf16[144,2,1728]{2,0,1:T(8,128)(2,1)} %collective-permute-done.5), channel_id=1, source_target_pairs={{0,4},{4,8},{8,12},{12,16},{16,20},{20,24},{24,28},{28,0},{1,5},{5... | collective-permute-start | bytes 2985992 | tf_op jit(solution)/shard_map/ppermute | solution.py:19
  245.3 156.9 %all-reduce.17.cloned.1.call-start = ((), (), s32[]{:S(2)}) async-start(), calls=%async_computation.7 | async-start | bytes 2359296 | tf_op jit(solution)/shard_map/psum | solution.py:171
  249.4 56.8 %collective-permute-start.6 = (bf16[144,2,1728]{2,0,1:T(8,128)(2,1)}, bf16[144,2,1728]{2,0,1:T(8,128)(2,1)}, u32[]{:S(2)}, u32[]{:S(2)}) collective-permute-start(bf16[144,2,1728]{2,0,1:T(8,128)(2,1)} %collective-permute-done.4), channel_id=1, source_target_pairs={{0,28},{4,0},{8,4},{12,8},{16,12},{20,16},{24,20},{28,24},{1,29},{... | collective-permute-start | bytes 2985992 | tf_op jit(solution)/shard_map/ppermute | solution.py:21
  269.7 42.0 %collective-permute-start.8 = (bf16[144,2,1728]{2,0,1:T(8,128)(2,1)}, bf16[144,2,1728]{2,0,1:T(8,128)(2,1)}, u32[]{:S(2)}, u32[]{:S(2)}) collective-permute-start(bf16[144,2,1728]{2,0,1:T(8,128)(2,1)} %collective-permute-done.7), channel_id=1, source_target_pairs={{0,4},{4,8},{8,12},{12,16},{16,20},{20,24},{24,28},{28,0},{1,5},{5... | collective-permute-start | bytes 2985992 | tf_op jit(solution)/shard_map/ppermute | solution.py:19
  351.4 176.2 %all-gather.10.cloned.1.call-start = ((), (), s32[]{:S(2)}) async-start(), calls=%async_computation.8 | async-start | bytes 9289728 | tf_op jit(solution)/shard_map/all_gather | solution.py:192
  352.0 222.9 %all-reduce.19.cloned.1.call-start = ((), (), s32[]{:S(2)}) async-start(), calls=%async_computation.9 | async-start | bytes 2359296 | tf_op jit(solution)/shard_map/psum | solution.py:195
  539.1 111.7 %all-reduce.23.cloned.1.call-start = ((), (), s32[]{:S(2)}) async-start(), calls=%async_computation.15 | async-start | bytes 3407872 | tf_op jit(solution)/shard_map/psum | solution.py:256
  590.0 15.5 %collective-permute-start.9 = (bf16[512,512]{0,1:T(8,128)(2,1)S(1)}, bf16[512,512]{0,1:T(8,128)(2,1)S(1)}, u32[]{:S(2)}, u32[]{:S(2)}) collective-permute-start(bf16[512,512]{0,1:T(8,128)(2,1)S(1)} %fusion.62), channel_id=1, source_target_pairs={{4,0},{8,4},{12,8},{5,1},{9,5},{13,9},{6,2},{10,6},{14,10},{7,3},{... | collective-permute-start | bytes 1572872 | tf_op jit(solution)/shard_map/ppermute | solution.py:30
  606.4 111.9 %reduce-scatter.15.cloned.1.call-start = ((), (), s32[]{:S(2)}) async-start(), calls=%async_computation.13 | async-start | bytes 73728
  655.6 124.8 %reduce-scatter.13.cloned.1.call-start = ((), (), s32[]{:S(2)}) async-start(), calls=%async_computation.12 | async-start | bytes 331776
  661.9 185.4 %reduce-scatter.9.cloned.1.call-start = ((), (), s32[]{:S(2)}) async-start(), calls=%async_computation.10 | async-start | bytes 1327104 | tf_op jit(solution)/shard_map/reduce_scatter | solution.py:271
  663.2 251.1 %reduce-scatter.11.cloned.1.call-start = ((), (), s32[]{:S(2)}) async-start(), calls=%async_computation.11 | async-start | bytes 1327104 | tf_op jit(solution)/shard_map/reduce_scatter | solution.py:289
  666.4 752.9 %all-reduce.21.cloned.1.call-start = ((), (), s32[]{:S(2)}) async-start(), calls=%async_computation.14 | async-start | bytes 33030144
  (77 other events, 612.9 us)
Sparse Core Ops, SparseCore 0:
  14.9 58.7 all-gather.5
  207.7 55.5 all-reduce.14
  265.4 79.5 all-gather.7
  351.6 50.5 all-reduce.16
  404.7 122.9 all-gather.9
  539.2 35.6 all-reduce.18
  606.6 44.1 all-reduce.22
  655.8 62.5 reduce-scatter.14
  722.2 58.1 reduce-scatter.12
  783.6 63.6 reduce-scatter.8
  850.7 63.5 reduce-scatter.10
  918.2 501.0 all-reduce.20
